TPU v7x, 512 devices: a whole 4x4x16 slice. The times are simulated.
512 devices in a mesh: seq: 64 (over x, z), head: 8 (over y, core).
Axes of the slice: x: 4, y: 4, z: 16, core: 2. Of those that a mesh axis runs over, the one named last changes fastest.
Arguments:
- queries: bfloat16 [16384, 4096], P('seq', 'head'), may hold values from -12 to 12
- key_input: bfloat16 [16384, 4096], P('seq', 'head'), may hold values from -1.796875 to 1.796875
- value_input: bfloat16 [16384, 4096], P('seq', 'head'), may hold values from -32 to 32
- norm_gain: bfloat16 [4096], P('head'), may hold values from 0.099609375 to 1.8984375
- out_weight: bfloat16 [4096, 3072], P('head', 'seq'), may hold values from -0.25 to 0.25
- target: bfloat16 [16384, 3072], P('seq', 'head'), may hold values from -6 to 6
Outputs:
- output: bfloat16 [16384, 3072], P('seq', 'head')
- query_grad: bfloat16 [16384, 4096], P('seq', 'head')
- key_grad: bfloat16 [16384, 4096], P('seq', 'head')
- value_grad: bfloat16 [16384, 4096], P('seq', 'head')
- gain_grads: float32 [64, 4096], P('seq', 'head')
- weight_grads: bfloat16 [64, 4096, 3072], P('seq', 'head')
All inputs are finite; a program needn't handle non-finite values.
Results may differ from a plain program's by a relative error of at most 0.022.
Values may be sent and summed in bfloat16 or wider, within the bound.
No kernel may reach another device: no remote copies, remote signals or barrier semaphores. Data moves between devices by JAX's collectives and lax.ppermute only.
A program may use at most 64 MiB of HBM per device.

v0:
```python
import jax
import jax.numpy as jnp
from jax import lax
from jax.sharding import Mesh
from jax.sharding import PartitionSpec as P

HEAD_DIM = 128
FEATURES = 4096
SEQ = ("seq_0", "seq_1")
EPSILON = 1e-06


def filled_with(shard, identity):
    return jnp.zeros_like(shard) + jnp.asarray(identity, shard.dtype)


def carried_in(shard, axes, combine, identity, reverse):
    before = start = filled_with(shard, identity)
    total = shard
    for axis in reversed(axes):
        length, index = (lax.axis_size(axis), lax.axis_index(axis))
        pieces = lax.all_gather(total.astype(jnp.bfloat16), axis)
        inside, total = (start, start)
        for k in reversed(range(length)) if reverse else range(length):
            passed = k > index if reverse else k < index
            total = combine(total, pieces[k].astype(shard.dtype))
            inside = jnp.where(passed, total, inside)
        before = combine(inside, before)
    return before


def laid_out(pieces, dim):
    pieces = jnp.moveaxis(pieces, 0, dim)
    dims = pieces.shape
    return pieces.reshape(*dims[:dim], dims[dim] * dims[dim + 1], *dims[dim + 2 :])


def gather_in_order(shard, axes, turns):
    pieces = shard[None]
    for k in turns:
        pieces = lax.all_gather(pieces, axes[k], axis=0, tiled=True)
    held = [lax.axis_size(axes[k]) for k in reversed(turns)]
    pieces = pieces.reshape(*held, *shard.shape)
    turned = sorted(range(len(turns)), key=lambda place: turns[len(turns) - 1 - place])
    return pieces.transpose(*turned, *range(len(turns), pieces.ndim)).reshape(-1, *shard.shape)


def gathered_by_axis(shard, axes, turns, dim):
    return laid_out(gather_in_order(shard, axes, turns), dim)


def in_blocks(shard, dim, length):
    before, after = (shard.shape[:dim], shard.shape[dim + 1 :])
    return jnp.moveaxis(shard.reshape(*before, length, -1, *after), dim, 0)


def summed_on_arrival(shard, axis, dim):
    length = lax.axis_size(axis)
    pieces = lax.all_to_all(in_blocks(shard, dim, length), axis, 0, 0, tiled=True)
    return jnp.sum(pieces.astype(jnp.float32), axis=0)


def causal(count):
    row_index = lax.broadcasted_iota(jnp.int32, (count, count), 0)
    col_index = lax.broadcasted_iota(jnp.int32, (count, count), 1)
    return row_index >= col_index


def add_states(earlier, later):
    return earlier + later


def per_device(queries, key_input, value_input, norm_gain, out_weight, target):
    tok_count = queries.shape[0]
    local_heads = queries.shape[1] // HEAD_DIM
    shape3 = (tok_count, local_heads, HEAD_DIM)
    q_heads = queries.reshape(shape3)
    k_heads = key_input.reshape(shape3)
    v_heads = value_input.reshape(shape3)
    keep_mask = causal(tok_count)
    f32 = jnp.float32
    state_local = jnp.einsum("shd,she->hde", k_heads, v_heads, preferred_element_type=f32)
    zero_state = jnp.zeros_like(state_local)
    earlier_state = carried_in(state_local, SEQ, add_states, zero_state, False)
    state_low = earlier_state.astype(jnp.bfloat16)
    scores = jnp.einsum("thd,shd->hts", q_heads, k_heads, preferred_element_type=f32)
    scores_low = jnp.where(keep_mask[None], scores, 0.0).astype(jnp.bfloat16)
    attended = jnp.einsum("hts,shd->thd", scores_low, v_heads, preferred_element_type=f32)
    attended = attended + jnp.einsum("thd,hde->the", q_heads, state_low, preferred_element_type=f32)
    mixed = attended.reshape(tok_count, -1)
    gain_float = norm_gain.astype(f32)
    squares = lax.psum(jnp.sum(mixed * mixed, axis=1, keepdims=True), "head")
    inverse = lax.rsqrt(squares / FEATURES + EPSILON)
    normed = (mixed * inverse * gain_float).astype(jnp.bfloat16)
    full_weight = gathered_by_axis(out_weight, SEQ, (0, 1), 1)
    partial_value = jnp.dot(normed, full_weight, preferred_element_type=f32)
    projected = summed_on_arrival(partial_value.astype(jnp.bfloat16), "head", 1)
    output = projected.astype(jnp.bfloat16)
    grad_local = (projected - target.astype(f32)).astype(jnp.bfloat16)
    out_grad = lax.all_gather(grad_local, "head", axis=1, tiled=True)
    normed_grad = lax.dot_general(
        out_grad, full_weight, (((1,), (1,)), ((), ())), preferred_element_type=f32
    )
    product = jnp.sum(grad_local.astype(f32) * projected, axis=1, keepdims=True)
    inner = lax.psum(product, "head") / inverse
    mixed_grad = inverse * gain_float * normed_grad - mixed * inverse**3 * inner / FEATURES
    mixed_grad = mixed_grad.astype(jnp.bfloat16)
    gain_grads = jnp.sum(normed_grad * mixed * inverse, axis=0)[None]
    weight_grads = lax.dot_general(
        normed, out_grad, (((0,), (0,)), ((), ())), preferred_element_type=f32
    ).astype(jnp.bfloat16)[None]
    grad_heads = mixed_grad.reshape(shape3)
    grad_state = jnp.einsum("thd,the->hde", q_heads, grad_heads, preferred_element_type=f32)
    later_state = carried_in(grad_state, SEQ, add_states, zero_state, True)
    later_low = later_state.astype(jnp.bfloat16)
    pairs = jnp.einsum("thd,shd->hts", grad_heads, v_heads, preferred_element_type=f32)
    pairs_low = jnp.where(keep_mask[None], pairs, 0.0).astype(jnp.bfloat16)
    query_grad = jnp.einsum("hts,shd->thd", pairs_low, k_heads, preferred_element_type=f32)
    query_grad = query_grad + jnp.einsum(
        "the,hde->thd", grad_heads, state_low, preferred_element_type=f32
    )
    key_grad = jnp.einsum("hts,thd->shd", pairs_low, q_heads, preferred_element_type=f32)
    key_grad = key_grad + jnp.einsum("she,hde->shd", v_heads, later_low, preferred_element_type=f32)
    value_grad = jnp.einsum("hts,the->she", scores_low, grad_heads, preferred_element_type=f32)
    value_grad = value_grad + jnp.einsum(
        "shd,hde->she", k_heads, later_low, preferred_element_type=f32
    )
    flat_shape = (tok_count, -1)
    return (
        output,
        query_grad.reshape(flat_shape).astype(jnp.bfloat16),
        key_grad.reshape(flat_shape).astype(jnp.bfloat16),
        value_grad.reshape(flat_shape).astype(jnp.bfloat16),
        gain_grads,
        weight_grads,
    )


def solution(mesh):
    torus = Mesh(mesh.devices.reshape(4, 16, mesh.shape["head"]), ("seq_0", "seq_1", "head"))
    return jax.shard_map(
        per_device,
        mesh=torus,
        in_specs=(
            P(SEQ, "head"),
            P(SEQ, "head"),
            P(SEQ, "head"),
            P("head"),
            P("head", SEQ),
            P(SEQ, "head"),
        ),
        out_specs=(
            P(SEQ, "head"),
            P(SEQ, "head"),
            P(SEQ, "head"),
            P(SEQ, "head"),
            P(SEQ, "head"),
            P(SEQ, "head", None),
        ),
        check_vma=False,
    )
```

profile of v0, /device:TPU:8, one launch (start us, length us, event | category | flops | bytes accessed | tf_op | source)
XLA Modules:
  0.0 324.0 jit_solution(6673106634308341939)
XLA Ops:
  7.3 1.1 copy.193
  8.4 1.9 convolution_convert_fusion.3
  10.4 12.7 %all-gather.1 = bf16[2048,48]{0,1:T(8,128)(2,1)S(1)} all-gather(bf16[512,48]{0,1:T(8,128)(2,1)} %param.10), channel_id=3, replica_groups=mesh['seq_0'=4,'seq_1'=16,'head'=8] {'seq_0'}, dimensions={0}, use_global_device_ids=true | all-gather | bytes 245760 | tf_op jit(solution)/shard_map/all_gather | solution.py:41
  25.7 62.0 %all-gather.12.cloned.1.call-done = bf16[64,128,128]{2,1,0:T(8,128)(2,1)} async-done(((bf16[4,128,128]{2,1,0:T(8,128)(2,1)}), bf16[64,128,128]{2,1,0:T(8,128)(2,1)}) %all-gather.12.cloned.1.call-update) | async-done | bytes 2097168 | tf_op jit(solution)/shard_map/all_gather | solution.py:22
  87.7 2.1 fusion.46
  89.8 13.1 %all_gather.31 = bf16[4,4,128,128]{3,2,1,0:T(8,128)(2,1)S(1)} all-gather(bf16[1,4,128,128]{3,2,1,0:T(8,128)(2,1)S(1)} %fusion.46), channel_id=1, replica_groups=mesh['seq_0'=4,'seq_1'=16,'head'=8] {'seq_0'}, dimensions={0}, use_global_device_ids=true | all-gather | bytes 655360 | tf_op jit(solution)/shard_map/all_gather | solution.py:22
  103.8 10.4 %psum.14 = f32[256,1]{0,1:T(1,128)S(1)} all-reduce(f32[256,1]{0,1:T(1,128)S(1)} %bitcast.395), channel_id=1, replica_groups=mesh['seq_0'=4,'seq_1'=16,'head'=8] {'head'}, use_global_device_ids=true, to_apply=%region_1.2 | all-reduce | flops 256 | bytes 2048 | tf_op jit(solution)/shard_map/psum | solution.py:92
  115.6 47.1 %all-gather.8.cloned.1.call-done = bf16[64,512,48]{1,2,0:T(8,128)(2,1)} async-done(((bf16[4,512,48]{1,2,0:T(8,128)(2,1)}), bf16[64,512,48]{1,2,0:T(8,128)(2,1)}) %all-gather.8.cloned.1.call-update) | async-done | bytes 3145744 | tf_op jit(solution)/shard_map/all_gather | solution.py:41
  162.7 2.2 copy.123
  164.9 1.0 convolution_convert_fusion.1
  166.2 25.0 %all_to_all.5 = bf16[8,256,384]{2,1,0:T(8,128)(2,1)S(1)} all-to-all(bf16[8,256,384]{2,1,0:T(8,128)(2,1)S(1)} %bitcast.376), channel_id=1, replica_groups=mesh['seq_0'=4,'seq_1'=16,'head'=8] {'head'}, dimensions={0} | all-to-all | bytes 3145728 | tf_op jit(solution)/shard_map/all_to_all | solution.py:59
  192.3 2.1 copy.125
  194.4 10.5 %psum.15 = f32[256,1]{0,1:T(1,128)S(1)} all-reduce(f32[256,1]{0,1:T(1,128)S(1)} %bitcast.394), channel_id=1, replica_groups=mesh['seq_0'=4,'seq_1'=16,'head'=8] {'head'}, use_global_device_ids=true, to_apply=%region_4.5 | all-reduce | flops 256 | bytes 2048 | tf_op jit(solution)/shard_map/psum | solution.py:105
  204.9 14.0 %all-gather.10.cloned.1.call-done = bf16[256,3072]{1,0:T(8,128)(2,1)} async-done(((bf16[256,384]{1,0:T(8,128)(2,1)}), bf16[256,3072]{1,0:T(8,128)(2,1)}) %all-gather.10.cloned.1.call-update) | async-done | bytes 1572880 | tf_op jit(solution)/shard_map/all_gather | solution.py:100
  218.9 3.9 %multiply_reduce_fusion = (f32[512]{0:T(512)}, bf16[256,512]{1,0:T(8,128)(2,1)}) fusion(f32[256,512]{1,0:T(8,128)} %copy.125, f32[256]{0:T(256)S(1)} %bitcast.392, f32[256]{0:T(256)S(1)} %bitcast.397, f32[256]{0:T(256)} %bitcast.396, f32[512]{0:T(512)S(1)} %get-tuple-element.43, bf16[256,3072]{1,0:T(8,128)(2,1)} %all-gather.10.cloned.1.call-done, ...), kind=kOutput, calls=%fused_computation.26 | convolution fusion | flops 806616576 | bytes 5512192 | tf_op jit(solution)/shard_map/dot_general | solution.py:101
  222.8 1.1 copy.145
  225.0 1.3 fusion.2
  226.9 0.8 copy.140
  227.7 4.2 %fusion = bf16[1,512,3072]{2,1,0:T(8,128)(2,1)} fusion(bf16[256,3072]{1,0:T(8,128)(2,1)} %all-gather.10.cloned.1.call-done, f32[256,512]{1,0:T(8,128)S(1)} %copy-done.4, f32[512]{0:T(512)S(1)} %get-tuple-element.43, f32[256]{0:T(256)S(1)} %bitcast.393), kind=kOutput, calls=%fused_computation.1 | convolution fusion | flops 807272448 | bytes 5245952 | tf_op jit(solution)/shard_map/dot_general | solution.py:109
  232.5 66.9 %all-gather.14.cloned.1.call-done = bf16[64,128,128]{2,1,0:T(8,128)(2,1)} async-done(((bf16[4,128,128]{2,1,0:T(8,128)(2,1)}), bf16[64,128,128]{2,1,0:T(8,128)(2,1)}) %all-gather.14.cloned.1.call-update) | async-done | bytes 2097168 | tf_op jit(solution)/shard_map/all_gather | solution.py:22
  299.3 2.1 fusion.71
  301.4 13.2 %all_gather.37 = bf16[4,4,128,128]{3,2,1,0:T(8,128)(2,1)S(1)} all-gather(bf16[1,4,128,128]{3,2,1,0:T(8,128)(2,1)S(1)} %fusion.71), channel_id=1, replica_groups=mesh['seq_0'=4,'seq_1'=16,'head'=8] {'seq_0'}, dimensions={0}, use_global_device_ids=true | all-gather | bytes 655360 | tf_op jit(solution)/shard_map/all_gather | solution.py:22
  315.5 0.8 copy.142
  316.6 0.8 copy.141
  (64 shorter events, 9.3 us)
Async XLA Ops:
  7.2 16.8 %copy-start = (bf16[256,512]{1,0:T(8,128)(2,1)S(1)}, bf16[256,512]{1,0:T(8,128)(2,1)}, u32[]{:S(2)}) copy-start(bf16[256,512]{1,0:T(8,128)(2,1)} %param.6) | copy-start | bytes 786436
  7.2 16.8 %copy-start.12 = (bf16[256,512]{1,0:T(8,128)(2,1)S(1)}, bf16[256,512]{1,0:T(8,128)(2,1)}, u32[]{:S(2)}) copy-start(bf16[256,512]{1,0:T(8,128)(2,1)} %param.7) | copy-start | bytes 786436
  7.2 18.2 %copy-start.7 = (bf16[256,512]{1,0:T(8,128)(2,1)S(1)}, bf16[256,512]{1,0:T(8,128)(2,1)}, u32[]{:S(2)}) copy-start(bf16[256,512]{1,0:T(8,128)(2,1)} %param.8) | copy-start | bytes 786436
  7.2 16.7 %copy-start.16 = (bf16[512]{0:T(512)(128)(2,1)S(1)}, bf16[512]{0:T(512)(128)(2,1)}, u32[]{:S(2)}) copy-start(bf16[512]{0:T(512)(128)(2,1)} %param.9) | copy-start | bytes 3076
  7.2 80.5 %all-gather.12.cloned.1.call-start = ((), (), s32[]{:S(2)}) async-start(), calls=%async_computation.3 | async-start | bytes 2228224 | tf_op jit(solution)/shard_map/all_gather | solution.py:22
  8.4 17.3 %copy-start.5 = (bf16[256,512]{0,1:T(8,128)(2,1)}, bf16[256,512]{0,1:T(8,128)(2,1)S(1)}, u32[]{:S(2)}) copy-start(bf16[256,512]{0,1:T(8,128)(2,1)S(1)} %copy.193) | copy-start | bytes 786436
  10.4 152.4 %all-gather.8.cloned.1.call-start = ((), (), s32[]{:S(2)}) async-start(), calls=%async_computation.1 | async-start | bytes 3342336 | tf_op jit(solution)/shard_map/all_gather | solution.py:41
  23.8 195.1 %all-gather.10.cloned.1.call-start = ((), (), s32[]{:S(2)}) async-start(), calls=%async_computation.2 | async-start | bytes 1769472 | tf_op jit(solution)/shard_map/all_gather | solution.py:100
  24.0 0.6 copy-start.15
  24.6 0.8 copy-start.9
  87.7 15.2 %copy-start.2 = (bf16[64,128,128]{2,1,0:T(8,128)(2,1)S(1)}, bf16[64,128,128]{2,1,0:T(8,128)(2,1)}, u32[]{:S(2)}) copy-start(bf16[64,128,128]{2,1,0:T(8,128)(2,1)} %all-gather.12.cloned.1.call-done) | copy-start | bytes 6291460
  103.7 59.0 %copy-start.3 = (f32[256,4,128]{0,2,1:T(8,128)}, f32[256,4,128]{0,2,1:T(8,128)S(1)}, u32[]{:S(2)}) copy-start(f32[256,4,128]{0,2,1:T(8,128)S(1)} %get-tuple-element.46) | copy-start | bytes 1572868
  162.7 2.2 copy-start.11
  166.2 25.3 %copy-start.14 = (bf16[256,384]{1,0:T(8,128)(2,1)S(1)}, bf16[256,384]{1,0:T(8,128)(2,1)}, u32[]{:S(2)}) copy-start(bf16[256,384]{1,0:T(8,128)(2,1)} %param.11) | copy-start | bytes 589828
  192.3 107.1 %all-gather.14.cloned.1.call-start = ((), (), s32[]{:S(2)}) async-start(), calls=%async_computation.4 | async-start | bytes 2228224 | tf_op jit(solution)/shard_map/all_gather | solution.py:22
  222.8 3.6 %copy-start.6 = (bf16[256,512]{0,1:T(8,128)(2,1)S(1)}, bf16[256,512]{0,1:T(8,128)(2,1)}, u32[]{:S(2)}) copy-start(bf16[256,512]{0,1:T(8,128)(2,1)} %copy-done.5) | copy-start | bytes 786436
  225.0 2.8 copy-start.4
  227.7 4.2 %copy-start.10 = (bf16[4,256,256]{2,1,0:T(8,128)(2,1)S(1)}, bf16[4,256,256]{2,1,0:T(8,128)(2,1)}, u32[]{:S(2)}) copy-start(bf16[4,256,256]{2,1,0:T(8,128)(2,1)} %copy-done.9) | copy-start | bytes 1572868
  299.3 15.3 %copy-start.1 = (bf16[64,128,128]{2,1,0:T(8,128)(2,1)S(1)}, bf16[64,128,128]{2,1,0:T(8,128)(2,1)}, u32[]{:S(2)}) copy-start(bf16[64,128,128]{2,1,0:T(8,128)(2,1)} %all-gather.14.cloned.1.call-done) | copy-start | bytes 6291460
  301.4 13.8 %copy-start.13 = (bf16[256,512]{1,0:T(8,128)(2,1)S(1)}, bf16[256,512]{1,0:T(8,128)(2,1)}, u32[]{:S(2)}) copy-start(bf16[256,512]{1,0:T(8,128)(2,1)} %param.7) | copy-start | bytes 786436
  314.6 1.7 copy-start.8
Sparse Core Ops, SparseCore 0:
  10.7 76.9 all-gather.11
  90.4 72.3 all-gather.7
  192.4 26.4 all-gather.9
  225.0 74.2 all-gather.13
where the time goes:
time: 324 us
  waiting for transfers between devices  190 us (59%)
  blocking collectives  84.9 us (26%)
  matrix products  15.1 us (5%)
  between operations  14.1 us (4%)
  local copies, waits for them, and re-layouts  11.9 us (4%)
  other arithmetic  7.74 us (2%)
    all_gather x2, waiting for transfers between devices, carried_in(): pieces = lax.all_gather(total.astype(jnp.bfloat16), axis)  129 us
    all_gather x1, waiting for transfers between devices, gather_in_order(): pieces = lax.all_gather(pieces, axes[k], axis=0, tiled=True)  47.1 us
    all_gather x2, blocking collectives, carried_in(): pieces = lax.all_gather(total.astype(jnp.bfloat16), axis)  26.3 us
    all_to_all x1, blocking collectives, summed_on_arrival(): lax.all_to_all(in_blocks(shard, dim, length), axis, 0, 0, tiled=True)  25 us
    all_gather x1, waiting for transfers between devices, per_device(): out_grad = lax.all_gather(grad_local, 'head', axis=1, tiled=True)  14 us
    all_gather x1, blocking collectives, gather_in_order(): pieces = lax.all_gather(pieces, axes[k], axis=0, tiled=True)  12.7 us
    psum x1, blocking collectives, per_device(): inner = lax.psum(product, 'head') / inverse  10.5 us
    psum x1, blocking collectives, per_device(): squares = lax.psum(jnp.sum(mixed * mixed, axis=1, keepdims=True), 'head')  10.4 us
  transfers between devices with their start and end apart: 4, of which 4 were waited for; matrix products, arithmetic and copies ran while one was open for 5% of the time, Pallas kernels for 0%

commit v1 on v0

--- a/solution.py
+++ b/solution.py
@@ -38,7 +38,10 @@
 def gather_in_order(shard, axes, turns):
     pieces = shard[None]
     for k in turns:
-        pieces = lax.all_gather(pieces, axes[k], axis=0, tiled=True)
+        devices = lax.axis_size(axes[k])
+        tiles = jnp.stack([pieces for _ in range(devices)])
+        tiles = lax.all_to_all(tiles, axes[k], split_axis=0, concat_axis=0)
+        pieces = jnp.concatenate(tiles, axis=0)
     held = [lax.axis_size(axes[k]) for k in reversed(turns)]
     pieces = pieces.reshape(*held, *shard.shape)
     turned = sorted(range(len(turns)), key=lambda place: turns[len(turns) - 1 - place])

time: 324 us -> 387 us (1.19)
  waiting for transfers between devices: 190 us -> 232 us
  starting transfers between devices: 0.16 us -> 15.5 us
    all_gather x2, waiting for transfers between devices: 129 us -> 216 us  [carried_in(): pieces = lax.all_gather(total.astype(jnp.bfloat16), axis)]
    all_gather x1 -> x0, waiting for transfers between devices: 47.1 us -> none  [gather_in_order(): pieces = lax.all_gather(pieces, axes[k], axis=0, tiled=True)]
    all_to_all x0 -> x1, starting transfers between devices: none -> 15.3 us  [gather_in_order(): tiles = lax.all_to_all(tiles, axes[k], split_axis=0, concat_axis=0)]
    all_gather x1 -> x0, blocking collectives: 12.7 us -> none  [gather_in_order(): pieces = lax.all_gather(pieces, axes[k], axis=0, tiled=True)]
    all_to_all x0 -> x1, blocking collectives: none -> 10.4 us  [gather_in_order(): tiles = lax.all_to_all(tiles, axes[k], split_axis=0, concat_axis=0)]
  transfers between devices with their start and end apart: 4 -> 4, of which waited for: 4 -> 3; matrix products, arithmetic and copies ran while one was open for 5% -> 6% of each run, Pallas kernels for 0% -> 0%
where the time goes in v1:
time: 387 us; the launch traced here: 386 us
  waiting for transfers between devices  232 us (60%)
  blocking collectives  83.7 us (22%)
  matrix products  18.5 us (5%)
  starting transfers between devices  15.5 us (4%)
  between operations  14.1 us (4%)
  local copies, waits for them, and re-layouts  13.7 us (4%)
  other arithmetic  8.77 us (2%)
    all_gather x2, waiting for transfers between devices, carried_in(): pieces = lax.all_gather(total.astype(jnp.bfloat16), axis)  216 us
    all_gather x2, blocking collectives, carried_in(): pieces = lax.all_gather(total.astype(jnp.bfloat16), axis)  26.8 us
    all_to_all x1, blocking collectives, summed_on_arrival(): lax.all_to_all(in_blocks(shard, dim, length), axis, 0, 0, tiled=True)  26 us
    all_gather x1, waiting for transfers between devices, per_device(): out_grad = lax.all_gather(grad_local, 'head', axis=1, tiled=True)  15.4 us
    all_to_all x1, starting transfers between devices, gather_in_order(): tiles = lax.all_to_all(tiles, axes[k], split_axis=0, concat_axis=0)  15.3 us
    psum x1, blocking collectives, per_device(): inner = lax.psum(product, 'head') / inverse  10.5 us
    all_to_all x1, blocking collectives, gather_in_order(): tiles = lax.all_to_all(tiles, axes[k], split_axis=0, concat_axis=0)  10.4 us
    psum x1, blocking collectives, per_device(): squares = lax.psum(jnp.sum(mixed * mixed, axis=1, keepdims=True), 'head')  9.99 us
  transfers between devices with their start and end apart: 4, of which 3 were waited for; matrix products, arithmetic and copies ran while one was open for 6% of the time, Pallas kernels for 0%

profile of v1, /device:TPU:8, one launch (start us, length us, event | category | flops | bytes accessed | tf_op | source)
XLA Modules:
  0.0 386.0 jit_solution(49492116282056873)
XLA Ops:
  8.0 10.4 %all_to_all.15 = bf16[4,1,512,48]{2,3,1,0:T(8,128)(2,1)S(1)} all-to-all(bf16[4,1,512,48]{2,3,1,0:T(8,128)(2,1)S(1)} %stack.6), channel_id=1, replica_groups=mesh['seq_0'=4,'seq_1'=16,'head'=8] {'seq_0'}, dimensions={0} | all-to-all | bytes 393216 | tf_op jit(solution)/shard_map/all_to_all | solution.py:43
  18.5 2.0 stack.7
  20.5 15.3 %all-to-all-start.1 = ((bf16[16,4,512,48]{2,3,1,0:T(8,128)(2,1)}), bf16[16,4,512,48]{2,3,1,0:T(8,128)(2,1)S(1)}, u32[]{:S(2)}, u32[]{:S(2)}) async-start(bf16[16,4,512,48]{2,3,1,0:T(8,128)(2,1)} %stack.7), calls=%async_computation.1 | async-start | bytes 6291456 | tf_op jit(solution)/shard_map/all_to_all | solution.py:43
  35.9 1.8 copy.138
  37.7 1.9 convolution_convert_fusion.3
  40.4 1.2 fusion.1
  42.4 2.1 convolution_bitcast_fusion.5
  44.5 149.5 %all-gather.8.cloned.1.call-done = bf16[64,128,128]{2,1,0:T(8,128)(2,1)} async-done(((bf16[4,128,128]{2,1,0:T(8,128)(2,1)}), bf16[64,128,128]{2,1,0:T(8,128)(2,1)}) %all-gather.8.cloned.1.call-update) | async-done | bytes 2097168 | tf_op jit(solution)/shard_map/all_gather | solution.py:22
  193.9 2.1 fusion.46
  196.0 13.6 %all_gather.25 = bf16[4,4,128,128]{3,2,1,0:T(8,128)(2,1)S(1)} all-gather(bf16[1,4,128,128]{3,2,1,0:T(8,128)(2,1)S(1)} %fusion.46), channel_id=1, replica_groups=mesh['seq_0'=4,'seq_1'=16,'head'=8] {'seq_0'}, dimensions={0}, use_global_device_ids=true | all-gather | bytes 655360 | tf_op jit(solution)/shard_map/all_gather | solution.py:22
  210.2 1.1 multiply_reduce_fusion.1
  211.3 10.0 %psum.14 = f32[256,1]{0,1:T(1,128)S(1)} all-reduce(f32[256,1]{0,1:T(1,128)S(1)} %bitcast.389), channel_id=1, replica_groups=mesh['seq_0'=4,'seq_1'=16,'head'=8] {'head'}, use_global_device_ids=true, to_apply=%region_1.2 | all-reduce | flops 256 | bytes 2048 | tf_op jit(solution)/shard_map/psum | solution.py:95
  221.8 1.9 multiply_convert_fusion.1
  225.9 26.0 %all_to_all.16 = bf16[8,256,384]{2,1,0:T(8,128)(2,1)S(1)} all-to-all(bf16[8,256,384]{2,1,0:T(8,128)(2,1)S(1)} %bitcast.372), channel_id=1, replica_groups=mesh['seq_0'=4,'seq_1'=16,'head'=8] {'head'}, dimensions={0} | all-to-all | bytes 3145728 | tf_op jit(solution)/shard_map/all_to_all | solution.py:62
  253.0 2.0 copy.72
  255.0 10.5 %psum.15 = f32[256,1]{0,1:T(1,128)S(1)} all-reduce(f32[256,1]{0,1:T(1,128)S(1)} %bitcast.388), channel_id=1, replica_groups=mesh['seq_0'=4,'seq_1'=16,'head'=8] {'head'}, use_global_device_ids=true, to_apply=%region_4.5 | all-reduce | flops 256 | bytes 2048 | tf_op jit(solution)/shard_map/psum | solution.py:108
  265.5 15.4 %all-gather.6.cloned.1.call-done = bf16[256,3072]{1,0:T(8,128)(2,1)} async-done(((bf16[256,384]{1,0:T(8,128)(2,1)}), bf16[256,3072]{1,0:T(8,128)(2,1)}) %all-gather.6.cloned.1.call-update) | async-done | bytes 1572880 | tf_op jit(solution)/shard_map/all_gather | solution.py:103
  280.9 3.9 %multiply_reduce_fusion = (f32[512]{0:T(512)}, bf16[256,512]{1,0:T(8,128)(2,1)}) fusion(f32[256,512]{1,0:T(8,128)} %copy.72, f32[256]{0:T(256)S(1)} %bitcast.386, f32[256]{0:T(256)S(1)} %bitcast.391, f32[256]{0:T(256)} %bitcast.390, f32[512]{0:T(512)S(1)} %get-tuple-element.31, bf16[256,3072]{1,0:T(8,128)(2,1)} %all-gather.6.cloned.1.call-done, ...), kind=kOutput, calls=%fused_computation.26 | convolution fusion | flops 806616576 | bytes 5512192 | tf_op jit(solution)/shard_map/dot_general | solution.py:104
  284.8 1.1 copy.92
  287.0 1.3 fusion.2
  289.8 4.2 %fusion = bf16[1,512,3072]{2,1,0:T(8,128)(2,1)} fusion(bf16[256,3072]{1,0:T(8,128)(2,1)} %all-gather.6.cloned.1.call-done, f32[256,512]{1,0:T(8,128)S(1)} %copy-done.5, f32[512]{0:T(512)S(1)} %get-tuple-element.31, f32[256]{0:T(256)S(1)} %bitcast.387), kind=kOutput, calls=%fused_computation.1 | convolution fusion | flops 807272448 | bytes 5245952 | tf_op jit(solution)/shard_map/dot_general | solution.py:112
  294.5 66.9 %all-gather.10.cloned.1.call-done = bf16[64,128,128]{2,1,0:T(8,128)(2,1)} async-done(((bf16[4,128,128]{2,1,0:T(8,128)(2,1)}), bf16[64,128,128]{2,1,0:T(8,128)(2,1)}) %all-gather.10.cloned.1.call-update) | async-done | bytes 2097168 | tf_op jit(solution)/shard_map/all_gather | solution.py:22
  361.4 2.1 fusion.71
  363.5 13.2 %all_gather.29 = bf16[4,4,128,128]{3,2,1,0:T(8,128)(2,1)S(1)} all-gather(bf16[1,4,128,128]{3,2,1,0:T(8,128)(2,1)S(1)} %fusion.71), channel_id=1, replica_groups=mesh['seq_0'=4,'seq_1'=16,'head'=8] {'seq_0'}, dimensions={0}, use_global_device_ids=true | all-gather | bytes 655360 | tf_op jit(solution)/shard_map/all_gather | solution.py:22
  (62 shorter events, 12.4 us)
Async XLA Ops:
  7.2 33.2 %copy-start = (bf16[256,512]{1,0:T(8,128)(2,1)S(1)}, bf16[256,512]{1,0:T(8,128)(2,1)}, u32[]{:S(2)}) copy-start(bf16[256,512]{1,0:T(8,128)(2,1)} %param.6) | copy-start | bytes 786436
  20.5 19.2 %copy-start.15 = (bf16[512]{0:T(512)(128)(2,1)S(1)}, bf16[512]{0:T(512)(128)(2,1)}, u32[]{:S(2)}) copy-start(bf16[512]{0:T(512)(128)(2,1)} %param.9) | copy-start | bytes 3076
  20.5 203.2 %all-to-all-start.1 = ((bf16[16,4,512,48]{2,3,1,0:T(8,128)(2,1)}), bf16[16,4,512,48]{2,3,1,0:T(8,128)(2,1)S(1)}, u32[]{:S(2)}, u32[]{:S(2)}) async-start(bf16[16,4,512,48]{2,3,1,0:T(8,128)(2,1)} %stack.7), calls=%async_computation.1 | async-start | bytes 6291456 | tf_op jit(solution)/shard_map/all_to_all | solution.py:43
  35.8 158.1 %all-gather.8.cloned.1.call-start = ((), (), s32[]{:S(2)}) async-start(), calls=%async_computation.4 | async-start | bytes 2228224 | tf_op jit(solution)/shard_map/all_gather | solution.py:22
  39.6 241.3 %all-gather.6.cloned.1.call-start = ((), (), s32[]{:S(2)}) async-start(), calls=%async_computation.3 | async-start | bytes 1769472 | tf_op jit(solution)/shard_map/all_gather | solution.py:103
  39.7 0.6 copy-start.14
  41.6 0.8 copy-start.8
  193.9 15.7 %copy-start.4 = (bf16[64,128,128]{2,1,0:T(8,128)(2,1)S(1)}, bf16[64,128,128]{2,1,0:T(8,128)(2,1)}, u32[]{:S(2)}) copy-start(bf16[64,128,128]{2,1,0:T(8,128)(2,1)} %all-gather.8.cloned.1.call-done) | copy-start | bytes 6291460
  196.0 14.2 %copy-start.10 = (f32[256,4,128]{0,2,1:T(8,128)S(1)}, f32[256,4,128]{0,2,1:T(8,128)}, u32[]{:S(2)}) copy-start(f32[256,4,128]{0,2,1:T(8,128)} %convolution_bitcast_fusion.5) | copy-start | bytes 1572868
  223.7 1.0 copy-start.11
  224.0 1.7 copy-start.1
  225.9 26.2 %copy-start.13 = (bf16[256,384]{1,0:T(8,128)(2,1)S(1)}, bf16[256,384]{1,0:T(8,128)(2,1)}, u32[]{:S(2)}) copy-start(bf16[256,384]{1,0:T(8,128)(2,1)} %param.11) | copy-start | bytes 589828
  251.9 29.0 %copy-start.2 = (bf16[16,4,512,48]{2,3,0,1:T(8,128)(2,1)S(1)}, bf16[16,4,512,48]{2,3,0,1:T(8,128)(2,1)}, u32[]{:S(2)}) copy-start(bf16[16,4,512,48]{2,3,0,1:T(8,128)(2,1)} %copy-done.1) | copy-start | bytes 9437188
  252.9 108.5 %all-gather.10.cloned.1.call-start = ((), (), s32[]{:S(2)}) async-start(), calls=%async_computation.5 | async-start | bytes 2228224 | tf_op jit(solution)/shard_map/all_gather | solution.py:22
  284.8 3.6 copy-start.6
  287.0 2.8 copy-start.5
  289.8 4.5 %copy-start.9 = (bf16[4,256,256]{2,1,0:T(8,128)(2,1)S(1)}, bf16[4,256,256]{2,1,0:T(8,128)(2,1)}, u32[]{:S(2)}) copy-start(bf16[4,256,256]{2,1,0:T(8,128)(2,1)} %copy-done.8) | copy-start | bytes 1572868
  361.4 15.3 %copy-start.3 = (bf16[64,128,128]{2,1,0:T(8,128)(2,1)S(1)}, bf16[64,128,128]{2,1,0:T(8,128)(2,1)}, u32[]{:S(2)}) copy-start(bf16[64,128,128]{2,1,0:T(8,128)(2,1)} %all-gather.10.cloned.1.call-done) | copy-start | bytes 6291460
  363.5 13.8 %copy-start.7 = (bf16[256,512]{1,0:T(8,128)(2,1)S(1)}, bf16[256,512]{1,0:T(8,128)(2,1)}, u32[]{:S(2)}) copy-start(bf16[256,512]{1,0:T(8,128)(2,1)} %param.8) | copy-start | bytes 786436
  376.7 1.7 copy-start.12
Sparse Core Ops, SparseCore 0:
  39.7 154.1 all-gather.7
  253.1 27.8 all-gather.5
  287.1 74.2 all-gather.9
